TPU v7x, 256 devices: a 2x2x32 block of a 4x8x32 slice. The times are simulated.
256 devices in a mesh: groups: 4 (over y, x), tp: 32 (over z), sp: 2 (over core).
Axes of the slice: x: 2, y: 2, z: 32, core: 2. Of those that a mesh axis runs over, the one named last changes fastest.
The devices are a block of a 4x8x32 slice.
Arguments:
- frames: bfloat16 [1024, 1280], P(('groups', 'tp', 'sp')), parts along dimension 0, may hold values from -6 to 6
- frame_pos: int32 [1024], P(('groups', 'tp', 'sp')), parts along dimension 0, may hold values from 0 to 511, as said below
- segment_ids: int32 [2048], P(('groups', 'sp')), parts along dimension 0, may hold values from 0 to 3, as said below
- text_embed: bfloat16 [2048, 8192], P(('groups', 'sp'), 'tp'), parts along dimension 0, may hold values from -6 to 6
- pre_gain: float32 [1280], replicated, may hold values from 0.25 to 1.75
- pre_shift: float32 [1280], replicated, may hold values from -1.75 to 1.75
- expand_weight: bfloat16 [1280, 5120], P(None, 'tp'), may hold values from -0.15625 to 0.15625
- expand_bias: float32 [5120], P('tp'), may hold values from -3 to 3
- reduce_weight: bfloat16 [5120, 1280], P('tp'), may hold values from -0.078125 to 0.078125
- reduce_bias: float32 [1280], replicated, may hold values from -3 to 3
- post_gain: float32 [1280], replicated, may hold values from 0.25 to 1.75
- post_shift: float32 [1280], replicated, may hold values from -1.75 to 1.75
- projector: bfloat16 [1280, 8192], P(None, 'tp'), may hold values from -0.15625 to 0.15625
- norm_gain: float32 [8192], P('tp'), may hold values from 0.5 to 12
- query_weight: bfloat16 [8192, 8192], P(None, 'tp'), may hold values from -0.0625 to 0.0625
- key_weight: bfloat16 [8192, 1024], P('tp'), may hold values from -0.0625 to 0.0625
- value_weight: bfloat16 [8192, 1024], P('tp'), may hold values from -0.0625 to 0.0625
- output_weight: bfloat16 [8192, 8192], P('tp'), may hold values from -1 to 1
Outputs:
- hidden_states: bfloat16 [2048, 8192], P(('groups', 'sp'), 'tp'), parts along dimension 0
There are 4 independent parts, one for each index of `groups`. A program takes and returns all parts, laid end to end along the dimension named above; an argument that names none is the same for every part. Nothing has to cross between parts.
Inputs may be any that keep to these rules, and one draw needn't show every extreme that they name: `frame_pos`: positions are distinct; each aligned run of 4 frame rows holds 4 consecutive positions starting at a multiple of 4. `segment_ids`: document numbers never fall along the prompt, and every number occurs.
All inputs are finite; a program needn't handle non-finite values.
Results may differ from a plain program's by a relative error of at most 0.034.
The roundings to bfloat16 on the way count: a program that leaves them out, or rounds other values in their place, can miss the bound.
Values may be sent and summed in bfloat16 or wider, within the bound.
No kernel may reach another device: no remote copies, remote signals or barrier semaphores. Data moves between devices by JAX's collectives and lax.ppermute only.
A program may use at most 64 MiB of HBM per device.

v0:
```python
import math

import jax
import jax.numpy as jnp
from jax import lax
from jax.sharding import PartitionSpec as P

D = 8192
NH = 64
KVH = 8
HD = 128


rope_base = 500000.0
norm_eps = 1e-05


def cut_along(value, dim, devices):
    shape = value.shape
    pieces = value.reshape(*shape[:dim], devices, shape[dim] // devices, *shape[dim + 1 :])
    return jnp.moveaxis(pieces, dim, 0)


def sent_and_summed(value, axis, dim):
    pieces = cut_along(value, dim, lax.axis_size(axis))
    arrived = lax.all_to_all(pieces, axis, split_axis=0, concat_axis=0, tiled=True)
    return arrived.sum(axis=0)


def in_order(pieces, dim):
    shape = list(pieces.shape[1:])
    shape[dim] *= pieces.shape[0]
    return jnp.moveaxis(pieces, 0, dim).reshape(shape)


def stacked_from(value, axes, turns):
    pieces = value
    for k in turns:
        pieces = lax.all_gather(pieces, axes[k])
    done = turns[::-1]
    back = [done.index(k) for k in range(len(axes))]
    pieces = pieces.transpose(*back, *range(len(axes), pieces.ndim))
    return pieces.reshape(-1, *value.shape)


def gather_axes(value, axes, turns, dim):
    return in_order(stacked_from(value, axes, turns), dim)


def from_everyone(value, axis):
    devices = lax.axis_size(axis)
    return lax.all_to_all(
        jnp.broadcast_to(value[None], (devices, *value.shape)), axis, 0, 0, tiled=True
    )


def taken_together(value, axis):
    everything = from_everyone(value, axis)
    return jnp.sum(everything, axis=0)


def layer_norm(values, gain, shift):
    widened = values.astype(jnp.float32)
    average = jnp.mean(widened, axis=-1, keepdims=True)
    centred = widened - average
    spread = jnp.mean(centred * centred, axis=-1, keepdims=True)
    return centred * lax.rsqrt(spread + norm_eps) * gain + shift


def rotate(values, positions):
    width = values.shape[-1]
    half_width = width // 2
    freq_index = jnp.arange(half_width).astype(jnp.float32)
    inverse = jnp.exp(freq_index * (-2.0 * math.log(rope_base) / width))
    angles = positions.astype(jnp.float32)[:, None] * inverse[None, :]
    cosine = jnp.cos(angles)[:, None, :]
    sine_part = jnp.sin(angles)[:, None, :]
    first = values[..., :half_width]
    second = values[..., half_width:]
    return jnp.concatenate(
        [first * cosine - second * sine_part, second * cosine + first * sine_part], axis=-1
    )


def per_device(
    frames,
    frame_pos,
    segment_ids,
    text_embed,
    pre_gain,
    pre_shift,
    expand_weight,
    expand_bias,
    reduce_weight,
    reduce_bias,
    post_gain,
    post_shift,
    projector,
    norm_gain,
    query_weight,
    key_weight,
    value_weight,
    output_weight,
):
    seq_rows = text_embed.shape[0]
    shard = lax.axis_index("sp")
    normed = layer_norm(frames, pre_gain, pre_shift).astype(jnp.bfloat16)
    inner = (
        jnp.dot(
            lax.all_gather(normed, "tp", axis=0, tiled=True),
            expand_weight,
            preferred_element_type=jnp.float32,
        )
        + expand_bias
    )
    inner_all = jax.nn.gelu(inner, approximate=False).astype(jnp.bfloat16)
    block = inner_all
    summed = sent_and_summed(
        jnp.dot(block, reduce_weight, preferred_element_type=jnp.float32), "tp", 0
    )
    encoded = frames.astype(jnp.float32) + summed + reduce_bias
    encoded = layer_norm(encoded, post_gain, post_shift).astype(jnp.bfloat16)
    audio, audio_pos = (
        gather_axes(encoded, ("tp", "sp"), (0, 1), 0),
        gather_axes(frame_pos, ("tp", "sp"), (0, 1), 0),
    )
    projected = jnp.dot(audio, projector, preferred_element_type=jnp.float32).astype(jnp.bfloat16)
    local_pos = audio_pos - shard * seq_rows
    row_ids = jnp.arange(seq_rows, dtype=jnp.int32)
    placing = row_ids[:, None] == local_pos[None, :]
    placed = jnp.dot(
        placing.astype(jnp.bfloat16), projected, preferred_element_type=jnp.float32
    ).astype(jnp.bfloat16)
    stream = jnp.where(jnp.any(placing, axis=1)[:, None], placed, text_embed)
    widened = stream.astype(jnp.float32)
    sum_squares = taken_together(jnp.sum(widened * widened, axis=1), "tp")
    normed_stream = (widened * lax.rsqrt(sum_squares[:, None] / D + norm_eps) * norm_gain).astype(
        jnp.bfloat16
    )
    key_part = jnp.dot(normed_stream, key_weight, preferred_element_type=jnp.float32)
    value_part = jnp.dot(normed_stream, value_weight, preferred_element_type=jnp.float32)
    key_total, value_total = lax.psum((key_part, value_part), "tp")
    query_raw = jnp.dot(
        lax.all_gather(normed_stream, "tp", axis=1, tiled=True),
        query_weight,
        preferred_element_type=jnp.float32,
    )
    positions = shard * seq_rows + jnp.arange(seq_rows, dtype=jnp.int32)
    heads_here = query_weight.shape[1] // HD
    queries = rotate(
        lax.optimization_barrier(query_raw.astype(jnp.bfloat16))
        .astype(jnp.float32)
        .reshape(seq_rows, heads_here, HD),
        positions,
    ).astype(jnp.bfloat16)
    shared_head = lax.axis_index("tp") * heads_here // (NH // KVH)
    key_mine = lax.dynamic_slice_in_dim(key_total, shared_head * HD, HD, 1).astype(jnp.bfloat16)
    value_mine = lax.dynamic_slice_in_dim(value_total, shared_head * HD, HD, 1).astype(jnp.bfloat16)
    key_rows = rotate(
        lax.optimization_barrier(key_mine).astype(jnp.float32)[:, None, :], positions
    )[:, 0, :].astype(jnp.bfloat16)
    inv_scale = 1.0 / math.sqrt(HD)
    running_max = jnp.full((heads_here, seq_rows), -1e30, jnp.float32)
    key_block = lax.all_gather(key_rows, "sp", axis=0, tiled=True)
    value_block = lax.all_gather(value_mine, "sp", axis=0, tiled=True)
    key_segs = lax.all_gather(segment_ids, "sp", axis=0, tiled=True)
    key_pos = jnp.arange(key_block.shape[0], dtype=jnp.int32)
    allowed = (key_pos[None, :] <= positions[:, None]) & (key_segs[None, :] == segment_ids[:, None])
    scores = (
        jnp.einsum("qhd,kd->hqk", queries, key_block, preferred_element_type=jnp.float32)
        * inv_scale
    )
    scores = jnp.where(allowed[None], scores, -1e30)
    new_max = jnp.maximum(running_max, jnp.max(scores, axis=2))
    expo = jnp.where(allowed[None], jnp.exp(scores - new_max[:, :, None]), 0.0)
    weight_sum = jnp.sum(expo, axis=2)
    accum = jnp.einsum(
        "hqk,kd->qhd", expo.astype(jnp.bfloat16), value_block, preferred_element_type=jnp.float32
    )
    running_max, weight_sum, accum = (new_max, weight_sum, accum)
    attended = (
        (accum / jnp.transpose(weight_sum)[:, :, None])
        .astype(jnp.bfloat16)
        .reshape(seq_rows, heads_here * HD)
    )
    block = output_weight
    mixed = jnp.transpose(
        lax.psum_scatter(
            jnp.einsum("hd,qh->dq", block, attended, preferred_element_type=jnp.float32).astype(
                jnp.bfloat16
            ),
            "tp",
            scatter_dimension=0,
            tiled=True,
        ).astype(jnp.float32)
    )
    return (widened + mixed).astype(jnp.bfloat16)


def solution(mesh):
    return jax.shard_map(
        per_device,
        mesh=mesh,
        in_specs=(
            P(("groups", "tp", "sp"), None),
            P(("groups", "tp", "sp")),
            P(("groups", "sp")),
            P(("groups", "sp"), "tp"),
            P(),
            P(),
            P(None, "tp"),
            P("tp"),
            P("tp", None),
            P(),
            P(),
            P(),
            P(None, "tp"),
            P("tp"),
            P(None, "tp"),
            P("tp", None),
            P("tp", None),
            P("tp", None),
        ),
        out_specs=P(("groups", "sp"), "tp"),
        check_vma=False,
    )
```

profile of v0, /device:TPU:38, one launch (start us, length us, event | category | flops | bytes accessed | tf_op | source)
XLA Modules:
  0.0 584.9 jit_solution(18425468708662384790)
XLA Ops:
  6.6 0.9 convert_reduce_fusion
  7.5 0.9 fusion.74
  8.4 0.8 fusion.80
  9.2 76.0 %all-gather.6 = bf16[32,4,1280]{2,1,0:T(4,128)(2,1)S(1)} all-gather(bf16[1,4,1280]{2,1,0:T(4,128)(2,1)S(1)} %fusion.80), channel_id=1, replica_groups=mesh['groups'=4,'tp'=32,'sp'=2] {'tp'}, dimensions={0}, use_global_device_ids=true | all-gather | bytes 337920 | tf_op jit(solution)/shard_map/all_gather | solution.py:110
  85.3 1.9 fusion.36
  87.2 1.0 reshape.223
  88.2 11.2 %all-to-all-start = ((f32[32,4,1280]{2,1,0:T(4,128)}), f32[32,4,1280]{2,1,0:T(4,128)S(1)}, u32[]{:S(2)}, u32[]{:S(2)}) async-start(f32[32,4,1280]{2,1,0:T(4,128)} %reshape.223), calls=%async_computation | async-start | bytes 1310720 | tf_op jit(solution)/shard_map/all_to_all | solution.py:26
  99.6 0.6 dynamic-slice
  101.1 67.1 %all-reduce = s32[128]{0:T(128)S(1)} all-reduce(s32[128]{0:T(128)S(1)} %dynamic-update-slice), channel_id=2, replica_groups=mesh['groups'=4,'tp'=32,'sp'=2] {'tp'}, use_global_device_ids=true, to_apply=%add | all-reduce | flops 128 | bytes 1024
  168.4 1.9 all-gather.5
  171.2 58.0 %all-gather.7 = bf16[32,4,1280]{2,1,0:T(4,128)(2,1)S(1)} all-gather(bf16[1,4,1280]{2,1,0:T(4,128)(2,1)S(1)} %fusion.79), channel_id=4, replica_groups=mesh['groups'=4,'tp'=32,'sp'=2] {'tp'}, dimensions={0}, use_global_device_ids=true | all-gather | bytes 337920 | tf_op jit(solution)/shard_map/all_gather | solution.py:39
  229.2 2.3 all-gather.3
  231.9 0.6 multiply_reduce_fusion
  232.5 42.3 %all_to_all.11 = f32[32,1,256]{2,1,0:T(1,128)S(1)} all-to-all(f32[32,1,256]{2,1,0:T(1,128)S(1)} %broadcast_in_dim.32), channel_id=1, replica_groups=mesh['groups'=4,'tp'=32,'sp'=2] {'tp'}, dimensions={0} | all-to-all | bytes 65536 | tf_op jit(solution)/shard_map/all_to_all | solution.py:52
  274.9 0.8 multiply_convert_fusion
  275.8 1.9 all-gather.8
  277.9 0.5 multiply_cosine_fusion
  278.4 1.3 fusion.118
  279.7 1.4 fusion.117
  281.1 148.8 %all-reduce.3 = (bf16[256,1024]{0,1:T(8,128)(2,1)}, bf16[256,1024]{1,0:T(8,128)(2,1)}) all-reduce(f32[256,1024]{0,1:T(8,128)S(1)} %fusion.118, f32[256,1024]{1,0:T(8,128)S(1)} %fusion.117), channel_id=1, replica_groups=mesh['groups'=4,'tp'=32,'sp'=2] {'tp'}, use_global_device_ids=true, to_apply=%region_9.10 | all-reduce | flops 524288 | bytes 3145728 | tf_op jit(solution)/shard_map/psum | solution.py:142
  429.9 0.8 dynamic-slice_convert_fusion
  431.1 2.0 all-gather.4
  433.1 0.8 dynamic-slice_convert_fusion.1
  433.9 2.1 all_gather.48
  436.0 4.8 convolution_convert_fusion.3
  441.4 0.4 fusion.116
  442.0 0.3 fusion.4
  442.3 0.8 copy-done.1
  443.1 3.8 fusion
  446.9 129.5 %reduce-scatter.2.cloned.1.call-done = bf16[256,256]{1,0:T(8,128)(2,1)} async-done(((bf16[8192,256]{1,0:T(8,128)(2,1)}), bf16[256,256]{1,0:T(8,128)(2,1)}) %reduce-scatter.2.cloned.1.call-update) | async-done | bytes 131088 | tf_op jit(solution)/shard_map/reduce_scatter | solution.py:188
  576.4 0.9 fusion.14
  577.3 0.8 copy.76
  (64 shorter events, 3.5 us)
Async XLA Ops:
  6.5 225.3 %copy-start = (bf16[1280,256]{1,0:T(8,128)(2,1)S(1)}, bf16[1280,256]{1,0:T(8,128)(2,1)}, u32[]{:S(2)}) copy-start(bf16[1280,256]{1,0:T(8,128)(2,1)} %param.30) | copy-start | bytes 1966084
  6.6 93.1 %copy-start.11 = (u32[256]{0:T(256)S(1)}, u32[256]{0:T(256)}, u32[]{:S(2)}) copy-start(u32[256]{0:T(256)} %constant.121) | copy-start | bytes 3076
  6.6 164.2 %copy-start.3 = (bf16[4,1280]{1,0:T(4,128)(2,1)S(1)}, bf16[4,1280]{1,0:T(4,128)(2,1)}, u32[]{:S(2)}) copy-start(bf16[4,1280]{1,0:T(4,128)(2,1)} %param.18) | copy-start | bytes 30724
  6.6 92.9 %copy-start.4 = (bf16[256,256]{1,0:T(8,128)(2,1)S(1)}, bf16[256,256]{1,0:T(8,128)(2,1)}, u32[]{:S(2)}) copy-start(bf16[256,256]{1,0:T(8,128)(2,1)} %param.21) | copy-start | bytes 393220
  6.6 94.3 %copy-start.10 = (s32[4]{0:T(128)S(1)}, s32[4]{0:T(128)}, u32[]{:S(2)}) copy-start(s32[4]{0:T(128)} %param.19) | copy-start | bytes 52
  6.6 164.2 %copy-start.5 = (f32[1280]{0:T(1024)S(1)}, f32[1280]{0:T(1024)}, u32[]{:S(2)}) copy-start(f32[1280]{0:T(1024)} %param.27) | copy-start | bytes 15364
  6.6 164.5 %copy-start.6 = (f32[1280]{0:T(1024)S(1)}, f32[1280]{0:T(1024)}, u32[]{:S(2)}) copy-start(f32[1280]{0:T(1024)} %param.29) | copy-start | bytes 15364
  6.6 164.5 %copy-start.7 = (f32[1280]{0:T(1024)S(1)}, f32[1280]{0:T(1024)}, u32[]{:S(2)}) copy-start(f32[1280]{0:T(1024)} %param.28) | copy-start | bytes 15364
  88.2 186.7 %copy-start.9 = (f32[256]{0:T(256)S(1)}, f32[256]{0:T(256)}, u32[]{:S(2)}) copy-start(f32[256]{0:T(256)} %param.31) | copy-start | bytes 3076
  88.2 187.6 %copy-start.8 = (s32[256]{0:T(256)S(1)}, s32[256]{0:T(256)}, u32[]{:S(2)}) copy-start(s32[256]{0:T(256)} %param.20) | copy-start | bytes 3076
  88.2 82.4 %all-to-all-start = ((f32[32,4,1280]{2,1,0:T(4,128)}), f32[32,4,1280]{2,1,0:T(4,128)S(1)}, u32[]{:S(2)}, u32[]{:S(2)}) async-start(f32[32,4,1280]{2,1,0:T(4,128)} %reshape.223), calls=%async_computation | async-start | bytes 1310720 | tf_op jit(solution)/shard_map/all_to_all | solution.py:26
  99.4 179.0 %copy-start.2 = (bf16[256,1024]{1,0:T(8,128)(2,1)S(1)}, bf16[256,1024]{1,0:T(8,128)(2,1)}, u32[]{:S(2)}) copy-start(bf16[256,1024]{1,0:T(8,128)(2,1)} %param.33) | copy-start | bytes 1572868
  99.4 336.6 %all-gather.11.cloned.1.call-start = ((), (), s32[]{:S(2)}) async-start(), calls=%async_computation.3 | async-start | bytes 4325376 | tf_op jit(solution)/shard_map/all_gather | solution.py:144
  275.7 300.7 %reduce-scatter.2.cloned.1.call-start = ((), (), s32[]{:S(2)}) async-start(), calls=%async_computation.4 | async-start | bytes 4325376 | tf_op jit(solution)/shard_map/reduce_scatter | solution.py:188
  440.9 2.2 copy-start.1
Sparse Core Ops, SparseCore 0:
  275.8 124.7 all-gather.10
  447.1 129.2 reduce-scatter.1
where the time goes:
time: 586 us; the launch traced here: 585 us
  blocking collectives  402 us (69%)
  waiting for transfers between devices  130 us (22%)
  matrix products  14.4 us (2%)
  between operations  14.4 us (2%)
  starting transfers between devices  11.3 us (2%)
  local copies, waits for them, and re-layouts  6.56 us (1%)
  other arithmetic  6.38 us (1%)
    psum x1, blocking collectives, per_device(): key_total, value_total = lax.psum((key_part, value_part), 'tp')  149 us
    reduce_scatter x1, waiting for transfers between devices, per_device(): lax.psum_scatter(jnp.einsum('hd,qh->dq', block, attended, preferred_eleme...  129 us
    all_gather x1, blocking collectives, per_device(): lax.all_gather(normed, 'tp', axis=0, tiled=True)  76 us
    unnamed x1, blocking collectives  67.1 us
    all_gather x3, blocking collectives, stacked_from(): pieces = lax.all_gather(pieces, axes[k])  62.1 us
    all_to_all x1, blocking collectives, from_everyone(): lax.all_to_all(jnp.broadcast_to(value[None], (devices, *value.shape)), ax...  42.3 us
  transfers between devices with their start and end apart: 3, of which 1 were waited for; matrix products, arithmetic and copies ran while one was open for 1% of the time, Pallas kernels for 0%

commit v1 on v0

v1 whole, which is shorter than its diff:
```python
import math

import jax
import jax.numpy as jnp
from jax import lax
from jax.experimental import pallas as pl
from jax.experimental.pallas import tpu as pltpu
from jax.sharding import PartitionSpec as P

D = 8192
NH = 64
KVH = 8
HD = 128


rope_base = 500000.0
norm_eps = 1e-05


def swapped(value):
    return lax.ppermute(value, "sp", [(0, 1), (1, 0)])


def in_three(values):
    high = lax.reduce_precision(values, 8, 7)
    middle = lax.reduce_precision(values - high, 8, 7)
    low = values - high - middle
    return jnp.stack([high, middle, low]).astype(jnp.bfloat16)


def query_kernel(width, rows, shard_ref, gathered, encoded, placing, is_audio, weight, query, squares):
    @pl.when(pl.program_id(0) == 0)
    def _():
        query[...] = jnp.zeros_like(query)
        squares[...] = jnp.zeros_like(squares)

    def both(first, last):
        return jnp.concatenate([gathered[0, first:last, :], gathered[1, first:last, :]], axis=1)

    projected = jnp.dot(
        encoded[...], both(0, width), preferred_element_type=jnp.float32
    ).astype(jnp.bfloat16)
    placed = jnp.dot(placing[...], projected, preferred_element_type=jnp.float32)
    text = both(width, width + rows).astype(jnp.float32)
    stream = jnp.where(is_audio[...] > 0.0, placed, text)
    half = squares.shape[1]
    squared = stream * stream
    squares[...] += squared[:, :half] + squared[:, half:]
    parts = both(width + rows, width + rows + 16).astype(jnp.float32)
    gain = parts[0:1] + parts[1:2] + parts[2:3]
    scaled = (stream * gain).astype(jnp.bfloat16)
    query[...] += jnp.dot(
        scaled, weight[...].reshape(scaled.shape[1], query.shape[1]), preferred_element_type=jnp.float32
    )


def query_partial(shard, gathered, encoded, placing, is_audio, weight):
    chips, height, half = gathered.shape
    frames, width = encoded.shape
    rows = placing.shape[0]
    columns = weight.shape[-1]
    grid_spec = pltpu.PrefetchScalarGridSpec(
        num_scalar_prefetch=1,
        grid=(chips // 2,),
        in_specs=[
            pl.BlockSpec((2, height, half), lambda g, s: (g, 0, 0)),
            pl.BlockSpec((frames, width), lambda g, s: (0, 0)),
            pl.BlockSpec((rows, frames), lambda g, s: (0, 0)),
            pl.BlockSpec((rows, 1), lambda g, s: (0, 0)),
            pl.BlockSpec((2, 1, half, columns), lambda g, s: (g, s[0], 0, 0)),
        ],
        out_specs=[
            pl.BlockSpec((rows, columns), lambda g, s: (0, 0)),
            pl.BlockSpec((rows, half), lambda g, s: (0, 0)),
        ],
    )
    features = chips * half
    return pl.pallas_call(
        lambda *refs: query_kernel(width, rows, *refs),
        grid_spec=grid_spec,
        out_shape=[
            jax.ShapeDtypeStruct((rows, columns), jnp.float32),
            jax.ShapeDtypeStruct((rows, half), jnp.float32),
        ],
        compiler_params=pltpu.CompilerParams(dimension_semantics=("arbitrary",)),
        cost_estimate=pl.CostEstimate(
            flops=2 * features * (frames * width + rows * frames + rows * columns),
            bytes_accessed=2 * gathered.size,
            transcendentals=0,
        ),
        name="query_partial",
    )(shard.reshape(1), gathered, encoded, placing, is_audio, weight)


def layer_norm(values, gain, shift):
    widened = values.astype(jnp.float32)
    average = jnp.mean(widened, axis=-1, keepdims=True)
    centred = widened - average
    spread = jnp.mean(centred * centred, axis=-1, keepdims=True)
    return centred * lax.rsqrt(spread + norm_eps) * gain + shift


def rotate(values, positions):
    width = values.shape[-1]
    half_width = width // 2
    freq_index = jnp.arange(half_width).astype(jnp.float32)
    inverse = jnp.exp(freq_index * (-2.0 * math.log(rope_base) / width))
    angles = positions.astype(jnp.float32)[:, None] * inverse[None, :]
    cosine = jnp.cos(angles)[:, None, :]
    sine_part = jnp.sin(angles)[:, None, :]
    first = values[..., :half_width]
    second = values[..., half_width:]
    return jnp.concatenate(
        [first * cosine - second * sine_part, second * cosine + first * sine_part], axis=-1
    )


def per_device(
    frames,
    frame_pos,
    segment_ids,
    text_embed,
    pre_gain,
    pre_shift,
    expand_weight,
    expand_bias,
    reduce_weight,
    reduce_bias,
    post_gain,
    post_shift,
    projector,
    norm_gain,
    query_weight,
    key_weight,
    value_weight,
    output_weight,
):
    seq_rows, width = text_embed.shape
    half = width // 2
    shard = lax.axis_index("sp").astype(jnp.int32)
    chips = lax.axis_size("tp")
    mine = lax.dynamic_slice_in_dim(text_embed, shard * half, half, 1)
    theirs = swapped(lax.dynamic_slice_in_dim(text_embed, (1 - shard) * half, half, 1))
    other_segs = swapped(segment_ids)
    low = shard == 0
    text_half = jnp.concatenate([jnp.where(low, mine, theirs), jnp.where(low, theirs, mine)])
    key_segs = jnp.concatenate(
        [jnp.where(low, segment_ids, other_segs), jnp.where(low, other_segs, segment_ids)]
    )
    gains = in_three(lax.dynamic_slice_in_dim(norm_gain, shard * half, half, 0))
    gathered = lax.all_gather(
        jnp.concatenate(
            [
                lax.dynamic_slice_in_dim(projector, shard * half, half, 1),
                text_half,
                jnp.pad(gains, ((0, 13), (0, 0))),
            ]
        ),
        "tp",
        axis=0,
    )
    normed = layer_norm(frames, pre_gain, pre_shift).astype(jnp.bfloat16)
    inner = (
        jnp.dot(
            lax.all_gather(normed, "tp", axis=0, tiled=True),
            expand_weight,
            preferred_element_type=jnp.float32,
        )
        + expand_bias
    )
    inner_all = jax.nn.gelu(inner, approximate=False).astype(jnp.bfloat16)
    parts = jnp.dot(inner_all, reduce_weight, preferred_element_type=jnp.float32).astype(
        jnp.bfloat16
    )
    arrived = lax.all_to_all(parts.reshape(chips, -1, parts.shape[1]), "tp", 0, 0, tiled=True)
    summed = arrived.astype(jnp.float32).sum(axis=0)
    encoded = frames.astype(jnp.float32) + summed + reduce_bias
    encoded = layer_norm(encoded, post_gain, post_shift).astype(jnp.bfloat16)
    enc_width = encoded.shape[1]
    where_to = jnp.stack([frame_pos // 256, frame_pos % 256], axis=1).astype(jnp.bfloat16)
    labelled = jnp.concatenate([encoded, jnp.pad(where_to, ((0, 0), (0, 126)))], axis=1)
    labelled = lax.all_gather(labelled, "tp", axis=0, tiled=True)
    labelled = lax.all_gather(labelled, "sp", axis=0, tiled=True)
    audio = labelled[:, :enc_width]
    pos_parts = labelled[:, enc_width : enc_width + 2].astype(jnp.float32)
    audio_pos = (pos_parts[:, 0] * 256.0 + pos_parts[:, 1]).astype(jnp.int32)
    projected = jnp.dot(audio, projector, preferred_element_type=jnp.float32).astype(jnp.bfloat16)
    positions = shard * seq_rows + jnp.arange(seq_rows, dtype=jnp.int32)
    placing = positions[:, None] == audio_pos[None, :]
    placed = jnp.dot(
        placing.astype(jnp.bfloat16), projected, preferred_element_type=jnp.float32
    ).astype(jnp.bfloat16)
    stream = jnp.where(jnp.any(placing, axis=1)[:, None], placed, text_embed)
    widened = stream.astype(jnp.float32)
    scaled = (widened * norm_gain).astype(jnp.bfloat16)
    key_part = jnp.dot(scaled, key_weight, preferred_element_type=jnp.float32)
    value_part = jnp.dot(scaled, value_weight, preferred_element_type=jnp.float32)
    key_total, value_total = lax.psum((key_part, value_part), "tp")
    shared_head = lax.axis_index("tp") * (query_weight.shape[1] // HD) // (NH // KVH)
    key_mine = lax.dynamic_slice_in_dim(key_total, shared_head * HD, HD, 1).astype(jnp.bfloat16)
    value_mine = lax.dynamic_slice_in_dim(value_total, shared_head * HD, HD, 1).astype(jnp.bfloat16)
    key_mine, value_mine, audio_pos, audio = lax.optimization_barrier(
        (key_mine, value_mine, audio_pos, audio)
    )
    all_rows = jnp.arange(key_segs.shape[0], dtype=jnp.int32)
    placing_all = all_rows[:, None] == audio_pos[None, :]
    is_audio = jnp.any(placing_all, axis=1)[:, None].astype(jnp.float32)
    heads_here = query_weight.shape[1] // HD
    query_sums, square_sums = query_partial(
        shard,
        gathered,
        audio,
        placing_all.astype(jnp.bfloat16),
        is_audio,
        query_weight.reshape(chips, 2, half, query_weight.shape[1]),
    )
    both_sums = jnp.concatenate([query_sums, square_sums], axis=1)
    own = lax.dynamic_slice_in_dim(both_sums, shard * seq_rows, seq_rows, 0)
    sent = lax.dynamic_slice_in_dim(both_sums, (1 - shard) * seq_rows, seq_rows, 0)
    own = own + swapped(sent)
    columns = query_weight.shape[1]
    inverse_rms = lax.rsqrt(jnp.sum(own[:, columns:], axis=1, keepdims=True) / D + norm_eps)
    query_raw = own[:, :columns] * inverse_rms
    queries = rotate(
        lax.optimization_barrier(query_raw.astype(jnp.bfloat16))
        .astype(jnp.float32)
        .reshape(seq_rows, heads_here, HD),
        positions,
    ).astype(jnp.bfloat16)
    key_mine = (key_mine.astype(jnp.float32) * inverse_rms).astype(jnp.bfloat16)
    value_mine = (value_mine.astype(jnp.float32) * inverse_rms).astype(jnp.bfloat16)
    key_rows = rotate(
        lax.optimization_barrier(key_mine).astype(jnp.float32)[:, None, :], positions
    )[:, 0, :].astype(jnp.bfloat16)
    both_rows = lax.all_gather(
        jnp.concatenate([key_rows, value_mine], axis=1), "sp", axis=0, tiled=True
    )
    key_block = both_rows[:, :HD]
    value_block = both_rows[:, HD:]
    inv_scale = 1.0 / math.sqrt(HD)
    running_max = jnp.full((heads_here, seq_rows), -1e30, jnp.float32)
    key_pos = jnp.arange(key_block.shape[0], dtype=jnp.int32)
    allowed = (key_pos[None, :] <= positions[:, None]) & (key_segs[None, :] == segment_ids[:, None])
    scores = (
        jnp.einsum("qhd,kd->hqk", queries, key_block, preferred_element_type=jnp.float32)
        * inv_scale
    )
    scores = jnp.where(allowed[None], scores, -1e30)
    new_max = jnp.maximum(running_max, jnp.max(scores, axis=2))
    expo = jnp.where(allowed[None], jnp.exp(scores - new_max[:, :, None]), 0.0)
    weight_sum = jnp.sum(expo, axis=2)
    accum = jnp.einsum(
        "hqk,kd->qhd", expo.astype(jnp.bfloat16), value_block, preferred_element_type=jnp.float32
    )
    running_max, weight_sum, accum = (new_max, weight_sum, accum)
    attended = (
        (accum / jnp.transpose(weight_sum)[:, :, None])
        .astype(jnp.bfloat16)
        .reshape(seq_rows, heads_here * HD)
    )
    block = output_weight
    mixed = jnp.transpose(
        lax.psum_scatter(
            jnp.einsum("hd,qh->dq", block, attended, preferred_element_type=jnp.float32).astype(
                jnp.bfloat16
            ),
            "tp",
            scatter_dimension=0,
            tiled=True,
        ).astype(jnp.float32)
    )
    return (widened + mixed).astype(jnp.bfloat16)


def solution(mesh):
    return jax.shard_map(
        per_device,
        mesh=mesh,
        in_specs=(
            P(("groups", "tp", "sp"), None),
            P(("groups", "tp", "sp")),
            P(("groups", "sp")),
            P(("groups", "sp"), "tp"),
            P(),
            P(),
            P(None, "tp"),
            P("tp"),
            P("tp", None),
            P(),
            P(),
            P(),
            P(None, "tp"),
            P("tp"),
            P(None, "tp"),
            P("tp", None),
            P("tp", None),
            P("tp", None),
        ),
        out_specs=P(("groups", "sp"), "tp"),
        check_vma=False,
    )
```

time: 586 us -> 525 us (0.90)
  blocking collectives: 402 us -> 281 us
  waiting for transfers between devices: 130 us -> 171 us
  Pallas kernels: 0 us -> 18.9 us
  matrix products: 14.4 us -> 7.12 us
    unnamed x1 -> x0, blocking collectives: 67.1 us -> none
    all_to_all x1 -> x0, blocking collectives: 42.3 us -> none  [from_everyone(): lax.all_to_all(jnp.broadcast_to(value[None], (devices, *value.shape)), ax...]
    all_to_all x1, waiting for transfers between devices: 0.01 us -> 40.8 us  [per_device(): lax.all_to_all(parts.reshape(chips, -1, parts.shape[1]), 'tp', 0, 0, tile...]
    pallas_call x0 -> x1, Pallas kernels: none -> 18.9 us  [query_partial(): pl.pallas_call(lambda *refs: query_kernel(width, rows, *refs), grid_spec=...]
    psum x1, blocking collectives: 149 us -> 139 us  [per_device(): key_total, value_total = lax.psum((key_part, value_part), 'tp')]
    dot_general x4 -> x3, matrix products: 9.34 us -> 2.62 us  [the longest x1 1.92 us: per_device(): jnp.dot(inner_all, reduce_weight, preferred_element_type=jnp.float32)]
    all_gather x6 -> x3, blocking collectives: 68.1 us -> 63.2 us  [the longest x1 58.6 us: per_device(): labelled = lax.all_gather(labelled, 'tp', axis=0, tiled=True)]
  transfers between devices with their start and end apart: 3 -> 6, of which waited for: 1 -> 4; matrix products, arithmetic and copies ran while one was open for 1% -> 3% of each run, Pallas kernels for 0% -> 4%
where the time goes in v1:
time: 525 us; the launch traced here: 524 us
  blocking collectives  281 us (54%)
  waiting for transfers between devices  171 us (33%)
  Pallas kernels  18.9 us (4%)
  between operations  13.9 us (3%)
  other arithmetic  12.1 us (2%)
  starting transfers between devices  11.8 us (2%)
  local copies, waits for them, and re-layouts  8.03 us (2%)
  matrix products  7.12 us (1%)
    psum x1, blocking collectives, per_device(): key_total, value_total = lax.psum((key_part, value_part), 'tp')  139 us
    reduce_scatter x1, waiting for transfers between devices, per_device(): lax.psum_scatter(jnp.einsum('hd,qh->dq', block, attended, preferred_eleme...  130 us
    all_gather x1, blocking collectives, per_device(): lax.all_gather(normed, 'tp', axis=0, tiled=True)  78.6 us
    all_gather x1, blocking collectives, per_device(): labelled = lax.all_gather(labelled, 'tp', axis=0, tiled=True)  58.6 us
    all_to_all x1, waiting for transfers between devices, per_device(): lax.all_to_all(parts.reshape(chips, -1, parts.shape[1]), 'tp', 0, 0, tile...  40.8 us
    pallas_call x1, Pallas kernels, query_partial(): pl.pallas_call(lambda *refs: query_kernel(width, rows, *refs), grid_spec=...  18.9 us
    all_to_all x1, starting transfers between devices, per_device(): lax.all_to_all(parts.reshape(chips, -1, parts.shape[1]), 'tp', 0, 0, tile...  11.4 us
  transfers between devices with their start and end apart: 6, of which 4 were waited for; matrix products, arithmetic and copies ran while one was open for 3% of the time, Pallas kernels for 4%

profile of v1, /device:TPU:38, one launch (start us, length us, event | category | flops | bytes accessed | tf_op | source)
XLA Modules:
  0.0 524.1 jit_solution(11469952186551161564)
XLA Ops:
  6.6 0.9 constant_dynamic-slice_fusion.1
  7.6 0.8 fusion.93
  8.4 0.4 collective-permute-done
  8.8 0.9 broadcast_select_fusion.1
  9.7 0.8 pad_maximum_fusion
  10.6 0.8 convert_reduce_fusion.1
  11.4 0.9 fusion.80
  12.3 0.8 fusion.87
  13.2 78.6 %all-gather.1 = bf16[32,4,1280]{2,1,0:T(4,128)(2,1)S(1)} all-gather(bf16[1,4,1280]{2,1,0:T(4,128)(2,1)S(1)} %fusion.87), channel_id=1, replica_groups=mesh['groups'=4,'tp'=32,'sp'=2] {'tp'}, dimensions={0}, use_global_device_ids=true | all-gather | bytes 337920 | tf_op jit(solution)/shard_map/all_gather | solution.py:165
  91.9 1.9 convolution_convert_fusion.1
  93.8 0.8 reshape.242
  94.7 11.4 %all-to-all-start = ((bf16[32,4,1280]{2,1,0:T(4,128)(2,1)}), bf16[32,4,1280]{2,1,0:T(4,128)(2,1)S(1)}, u32[]{:S(2)}, u32[]{:S(2)}) async-start(bf16[32,4,1280]{2,1,0:T(4,128)(2,1)} %reshape.242), calls=%async_computation | async-start | bytes 655360 | tf_op jit(solution)/shard_map/all_to_all | solution.py:175
  106.5 1.2 multiply_cosine_fusion
  107.7 40.8 %all-to-all-done = bf16[32,4,1280]{2,1,0:T(4,128)(2,1)S(1)} async-done(((bf16[32,4,1280]{2,1,0:T(4,128)(2,1)}), bf16[32,4,1280]{2,1,0:T(4,128)(2,1)S(1)}, u32[]{:S(2)}, u32[]{:S(2)}) %all-to-all-start) | async-done | bytes 327712 | tf_op jit(solution)/shard_map/all_to_all | solution.py:175
  149.2 58.6 %all-gather.2 = bf16[32,4,1408]{2,1,0:T(4,128)(2,1)S(1)} all-gather(bf16[1,4,1408]{2,1,0:T(4,128)(2,1)S(1)} %fusion.86), channel_id=1, replica_groups=mesh['groups'=4,'tp'=32,'sp'=2] {'tp'}, dimensions={0}, use_global_device_ids=true | all-gather | bytes 371712 | tf_op jit(solution)/shard_map/all_gather | solution.py:182
  207.9 2.4 all_gather.20
  210.3 0.9 slice.51.refs_2_
  211.5 0.6 fusion.6
  212.8 139.0 %all-reduce.4 = (bf16[256,1024]{0,1:T(8,128)(2,1)S(1)}, bf16[256,1024]{0,1:T(8,128)(2,1)}) all-reduce(f32[256,1024]{0,1:T(8,128)S(1)} %fusion.45, f32[256,1024]{0,1:T(8,128)S(1)} %fusion.44), channel_id=1, replica_groups=mesh['groups'=4,'tp'=32,'sp'=2] {'tp'}, use_global_device_ids=true, to_apply=%region_6.7 | all-reduce | flops 524288 | bytes 3145728 | tf_op jit(solution)/shard_map/psum | solution.py:198
  351.8 0.8 dynamic-slice_convert_fusion
  352.7 0.8 fusion.12
  353.5 0.9 copy.45.refs_4_
  354.3 18.9 %query_partial.1 = (f32[512,256]{1,0:T(8,128)}, f32[512,128]{1,0:T(8,128)}) custom-call(s32[1]{0:T(128)} %bitcast.4.refs_0_, bf16[32,1808,128]{2,1,0:T(8,128)(2,1)} %bitcast.57, bf16[256,1280]{1,0:T(8,128)(2,1)} %slice.51.refs_2_, bf16[512,256]{1,0:T(8,128)(2,1)} %get-tuple-element.34.refs_3_, f32[512,1]{1,0:T(8,128)} %copy.45.refs_4_, ...), custom_call_target="tpu_custom_call" | custom-call | flops 4831838208 | bytes 14811136 | tf_op jit(solution)/shard_map/query_partial/pallas_call | solution.py:78
  373.3 1.1 constant_dynamic-update-slice_fusion.1
  374.4 1.0 constant_dynamic-update-slice_fusion
  375.6 0.7 broadcast_select_fusion.3
  376.3 0.9 fusion.14
  378.0 2.2 all_gather.23
  381.8 0.8 copy-done.1
  382.6 3.2 fusion
  385.8 129.9 %reduce-scatter.2.cloned.1.call-done = bf16[256,256]{0,1:T(8,128)(2,1)} async-done(((bf16[8192,256]{0,1:T(8,128)(2,1)}), bf16[256,256]{0,1:T(8,128)(2,1)}) %reduce-scatter.2.cloned.1.call-update) | async-done | bytes 131088 | tf_op jit(solution)/shard_map/reduce_scatter | solution.py:263
  515.7 1.6 fusion.18
  (82 shorter events, 4.9 us)
Async XLA Ops:
  6.5 1.8 copy-start
  6.6 142.2 %copy-start.6 = (bf16[4,1280]{1,0:T(4,128)(2,1)S(1)}, bf16[4,1280]{1,0:T(4,128)(2,1)}, u32[]{:S(2)}) copy-start(bf16[4,1280]{1,0:T(4,128)(2,1)} %param.18) | copy-start | bytes 30724
  6.6 99.8 %copy-start.14 = (s32[4]{0:T(128)S(1)}, s32[4]{0:T(128)}, u32[]{:S(2)}) copy-start(s32[4]{0:T(128)} %param.19) | copy-start | bytes 52
  6.6 142.2 %copy-start.8 = (f32[1280]{0:T(1024)S(1)}, f32[1280]{0:T(1024)}, u32[]{:S(2)}) copy-start(f32[1280]{0:T(1024)} %param.27) | copy-start | bytes 15364
  6.6 142.5 %copy-start.10 = (f32[1280]{0:T(1024)S(1)}, f32[1280]{0:T(1024)}, u32[]{:S(2)}) copy-start(f32[1280]{0:T(1024)} %param.28) | copy-start | bytes 15364
  6.6 142.5 %copy-start.9 = (f32[1280]{0:T(1024)S(1)}, f32[1280]{0:T(1024)}, u32[]{:S(2)}) copy-start(f32[1280]{0:T(1024)} %param.29) | copy-start | bytes 15364
  6.6 347.8 %all-gather.5.cloned.1.call-start = ((), (), s32[]{:S(2)}) async-start(), calls=%async_computation.3 | async-start | bytes 15273984 | tf_op jit(solution)/shard_map/all_gather | solution.py:151
  7.6 1.3 collective-permute-start
  91.9 119.7 %copy-start.7 = (bf16[256,256]{1,0:T(8,128)(2,1)S(1)}, bf16[256,256]{1,0:T(8,128)(2,1)}, u32[]{:S(2)}) copy-start(bf16[256,256]{1,0:T(8,128)(2,1)} %param.21) | copy-start | bytes 393220
  93.8 118.3 %copy-start.2 = (bf16[256,1024]{1,0:T(8,128)(2,1)S(1)}, bf16[256,1024]{1,0:T(8,128)(2,1)}, u32[]{:S(2)}) copy-start(bf16[256,1024]{1,0:T(8,128)(2,1)} %param.34) | copy-start | bytes 1572868
  93.8 118.3 %copy-start.11 = (f32[256]{0:T(256)S(1)}, f32[256]{0:T(256)}, u32[]{:S(2)}) copy-start(f32[256]{0:T(256)} %param.31) | copy-start | bytes 3076
  94.7 53.9 %all-to-all-start = ((bf16[32,4,1280]{2,1,0:T(4,128)(2,1)}), bf16[32,4,1280]{2,1,0:T(4,128)(2,1)S(1)}, u32[]{:S(2)}, u32[]{:S(2)}) async-start(bf16[32,4,1280]{2,1,0:T(4,128)(2,1)} %reshape.242), calls=%async_computation | async-start | bytes 655360 | tf_op jit(solution)/shard_map/all_to_all | solution.py:175
  106.1 409.6 %reduce-scatter.2.cloned.1.call-start = ((), (), s32[]{:S(2)}) async-start(), calls=%async_computation.2 | async-start | bytes 4325376 | tf_op jit(solution)/shard_map/reduce_scatter | solution.py:263
  106.2 269.4 %collective-permute-start.2 = (s32[256]{0:T(256)}, s32[256]{0:T(256)}, u32[]{:S(2)}, u32[]{:S(2)}) collective-permute-start(s32[256]{0:T(256)} %param.20), channel_id=1, source_target_pairs={{0,1},{1,0},{2,3},{3,2},{4,5},{5,4},{6,7},{7,6},{8,9},{9,8},{10,11... | collective-permute-start | bytes 3080 | tf_op jit(solution)/shard_map/ppermute | solution.py:21
  106.5 1.3 copy-start.12
  107.7 104.7 %copy-start.3 = (bf16[256,1024]{1,0:T(8,128)(2,1)S(1)}, bf16[256,1024]{1,0:T(8,128)(2,1)}, u32[]{:S(2)}) copy-start(bf16[256,1024]{1,0:T(8,128)(2,1)} %param.33) | copy-start | bytes 1572868
  373.3 4.3 copy-start.13
  373.3 7.4 %copy-start.4 = (f32[256,64]{1,0:T(8,128)S(1)}, f32[256,64]{1,0:T(8,128)}, u32[]{:S(2)}) copy-start(f32[256,64]{1,0:T(8,128)} %get-tuple-element.29) | copy-start | bytes 196612
  373.3 7.4 %copy-start.5 = (f32[256,64]{1,0:T(8,128)S(1)}, f32[256,64]{1,0:T(8,128)}, u32[]{:S(2)}) copy-start(f32[256,64]{1,0:T(8,128)} %get-tuple-element.30) | copy-start | bytes 196612
  375.4 1.8 collective-permute-start.1
  380.4 2.2 copy-start.1
Sparse Core Ops, SparseCore 0:
  10.7 235.3 all-gather.4
  385.9 129.7 reduce-scatter.1

commit v2 on v1

--- a/solution.py
+++ b/solution.py
@@ -172,6 +172,15 @@
     parts = jnp.dot(inner_all, reduce_weight, preferred_element_type=jnp.float32).astype(
         jnp.bfloat16
     )
+    parts, key_weight, value_weight = lax.optimization_barrier((parts, key_weight, value_weight))
+    by_head = jnp.concatenate(
+        [
+            weight[:, k * HD : (k + 1) * HD]
+            for k in range(KVH)
+            for weight in (key_weight, value_weight)
+        ],
+        axis=1,
+    )
     arrived = lax.all_to_all(parts.reshape(chips, -1, parts.shape[1]), "tp", 0, 0, tiled=True)
     summed = arrived.astype(jnp.float32).sum(axis=0)
     encoded = frames.astype(jnp.float32) + summed + reduce_bias
@@ -179,6 +188,7 @@
     enc_width = encoded.shape[1]
     where_to = jnp.stack([frame_pos // 256, frame_pos % 256], axis=1).astype(jnp.bfloat16)
     labelled = jnp.concatenate([encoded, jnp.pad(where_to, ((0, 0), (0, 126)))], axis=1)
+    labelled, by_head = lax.optimization_barrier((labelled, by_head))
     labelled = lax.all_gather(labelled, "tp", axis=0, tiled=True)
     labelled = lax.all_gather(labelled, "sp", axis=0, tiled=True)
     audio = labelled[:, :enc_width]
@@ -193,12 +203,20 @@
     stream = jnp.where(jnp.any(placing, axis=1)[:, None], placed, text_embed)
     widened = stream.astype(jnp.float32)
     scaled = (widened * norm_gain).astype(jnp.bfloat16)
-    key_part = jnp.dot(scaled, key_weight, preferred_element_type=jnp.float32)
-    value_part = jnp.dot(scaled, value_weight, preferred_element_type=jnp.float32)
-    key_total, value_total = lax.psum((key_part, value_part), "tp")
-    shared_head = lax.axis_index("tp") * (query_weight.shape[1] // HD) // (NH // KVH)
-    key_mine = lax.dynamic_slice_in_dim(key_total, shared_head * HD, HD, 1).astype(jnp.bfloat16)
-    value_mine = lax.dynamic_slice_in_dim(value_total, shared_head * HD, HD, 1).astype(jnp.bfloat16)
+    sharers = chips // KVH
+    quads = [[sharers * k + m for m in range(sharers)] for k in range(KVH)]
+    strides = [[sharers * k + m for k in range(KVH)] for m in range(sharers)]
+    shared = jnp.dot(scaled, by_head, preferred_element_type=jnp.float32).astype(jnp.bfloat16)
+    shared = lax.all_to_all(
+        shared.reshape(sharers, seq_rows // sharers, -1), "tp", 0, 0, axis_index_groups=quads, tiled=True
+    )
+    shared = shared.astype(jnp.float32).sum(axis=0).astype(jnp.bfloat16)
+    shared = jnp.transpose(shared.reshape(seq_rows // sharers, KVH, 2 * HD), (1, 0, 2))
+    shared = lax.all_to_all(shared, "tp", 0, 0, axis_index_groups=strides, tiled=True)
+    shared = shared.astype(jnp.float32).sum(axis=0).astype(jnp.bfloat16)
+    shared = lax.all_gather(shared, "tp", axis=0, tiled=True, axis_index_groups=quads)
+    key_mine = shared[:, :HD]
+    value_mine = shared[:, HD:]
     key_mine, value_mine, audio_pos, audio = lax.optimization_barrier(
         (key_mine, value_mine, audio_pos, audio)
     )

time: 525 us -> 480 us (0.914)
  blocking collectives: 281 us -> 201 us
  waiting for transfers between devices: 171 us -> 201 us
  starting transfers between devices: 11.8 us -> 18.7 us
    psum x1 -> x0, blocking collectives: 139 us -> none  [per_device(): key_total, value_total = lax.psum((key_part, value_part), 'tp')]
    all_to_all x0 -> x1, blocking collectives: none -> 40.5 us  [per_device(): lax.all_to_all(shared.reshape(sharers, seq_rows // sharers, -1), 'tp', 0,...]
    all_to_all x0 -> x1, waiting for transfers between devices: none -> 31 us  [per_device(): lax.all_to_all(shared, 'tp', 0, 0, axis_index_groups=strides, tiled=True)]
    all_gather x0 -> x1, blocking collectives: none -> 18.2 us  [per_device(): lax.all_gather(shared, 'tp', axis=0, tiled=True, axis_index_groups=quads)]
    all_to_all x0 -> x1, starting transfers between devices: none -> 6.93 us  [per_device(): lax.all_to_all(shared, 'tp', 0, 0, axis_index_groups=strides, tiled=True)]
  transfers between devices with their start and end apart: 6 -> 7, of which waited for: 4 -> 5; matrix products, arithmetic and copies ran while one was open for 3% -> 3% of each run, Pallas kernels for 4% -> 4%
where the time goes in v2:
time: 480 us; the launch traced here: 479 us
  waiting for transfers between devices  201 us (42%)
  blocking collectives  201 us (42%)
  Pallas kernels  18.9 us (4%)
  starting transfers between devices  18.7 us (4%)
  between operations  13.9 us (3%)
  other arithmetic  10.3 us (2%)
  local copies, waits for them, and re-layouts  8.92 us (2%)
  matrix products  6.87 us (1%)
    reduce_scatter x1, waiting for transfers between devices, per_device(): lax.psum_scatter(jnp.einsum('hd,qh->dq', block, attended, preferred_eleme...  126 us
    all_gather x1, blocking collectives, per_device(): lax.all_gather(normed, 'tp', axis=0, tiled=True)  78.6 us
    all_gather x1, blocking collectives, per_device(): labelled = lax.all_gather(labelled, 'tp', axis=0, tiled=True)  58.7 us
    all_to_all x1, waiting for transfers between devices, per_device(): lax.all_to_all(parts.reshape(chips, -1, parts.shape[1]), 'tp', 0, 0, tile...  41.7 us
    all_to_all x1, blocking collectives, per_device(): lax.all_to_all(shared.reshape(sharers, seq_rows // sharers, -1), 'tp', 0,...  40.5 us
    all_to_all x1, waiting for transfers between devices, per_device(): lax.all_to_all(shared, 'tp', 0, 0, axis_index_groups=strides, tiled=True)  31 us
    pallas_call x1, Pallas kernels, query_partial(): pl.pallas_call(lambda *refs: query_kernel(width, rows, *refs), grid_spec=...  18.9 us
    all_gather x1, blocking collectives, per_device(): lax.all_gather(shared, 'tp', axis=0, tiled=True, axis_index_groups=quads)  18.2 us
  transfers between devices with their start and end apart: 7, of which 5 were waited for; matrix products, arithmetic and copies ran while one was open for 3% of the time, Pallas kernels for 4%

profile of v2, /device:TPU:38, one launch (start us, length us, event | category | flops | bytes accessed | tf_op | source)
XLA Modules:
  0.0 479.0 jit_solution(13430244061450958140)
XLA Ops:
  6.6 1.0 constant_dynamic-slice_fusion.1
  7.6 0.8 fusion.91
  8.8 0.9 broadcast_select_fusion.1
  9.7 0.8 pad_maximum_fusion
  10.6 0.8 convert_reduce_fusion.1
  11.4 0.9 fusion.79
  12.3 0.8 fusion.85
  13.2 78.6 %all-gather.1 = bf16[32,4,1280]{2,1,0:T(4,128)(2,1)S(1)} all-gather(bf16[1,4,1280]{2,1,0:T(4,128)(2,1)S(1)} %fusion.85), channel_id=1, replica_groups=mesh['groups'=4,'tp'=32,'sp'=2] {'tp'}, dimensions={0}, use_global_device_ids=true | all-gather | bytes 337920 | tf_op jit(solution)/shard_map/all_gather | solution.py:165
  91.9 1.9 convolution_convert_fusion.2
  93.8 0.8 reshape.248
  94.6 11.4 %all-to-all-start = ((bf16[32,4,1280]{2,1,0:T(4,128)(2,1)}), bf16[32,4,1280]{2,1,0:T(4,128)(2,1)S(1)}, u32[]{:S(2)}, u32[]{:S(2)}) async-start(bf16[32,4,1280]{2,1,0:T(4,128)(2,1)} %reshape.248), calls=%async_computation | async-start | bytes 655360 | tf_op jit(solution)/shard_map/all_to_all | solution.py:184
  106.8 41.7 %all-to-all-done = bf16[32,4,1280]{2,1,0:T(4,128)(2,1)S(1)} async-done(((bf16[32,4,1280]{2,1,0:T(4,128)(2,1)}), bf16[32,4,1280]{2,1,0:T(4,128)(2,1)S(1)}, u32[]{:S(2)}, u32[]{:S(2)}) %all-to-all-start) | async-done | bytes 327712 | tf_op jit(solution)/shard_map/all_to_all | solution.py:184
  149.1 58.7 %all-gather.2 = bf16[32,4,1408]{2,1,0:T(4,128)(2,1)S(1)} all-gather(bf16[1,4,1408]{2,1,0:T(4,128)(2,1)S(1)} %bitcast.66), channel_id=1, replica_groups=mesh['groups'=4,'tp'=32,'sp'=2] {'tp'}, dimensions={0}, use_global_device_ids=true | all-gather | bytes 371712 | tf_op jit(solution)/shard_map/all_gather | solution.py:192
  207.9 2.4 all_gather.23
  210.7 0.6 fusion.6
  212.0 40.5 %all_to_all.15 = bf16[4,64,2048]{2,1,0:T(8,128)(2,1)S(1)} all-to-all(bf16[4,64,2048]{2,1,0:T(8,128)(2,1)S(1)} %bitcast.61), channel_id=1, replica_groups={{0,2,4,6},{8,10,12,14},{16,18,20,22},{24,26,28,30},{32,34,36,38},{40,42..., dimensions={0} | all-to-all | bytes 2097152 | tf_op jit(solution)/shard_map/all_to_all | solution.py:210
  252.8 0.8 copy.58
  253.5 6.9 %all-to-all-start.2 = ((bf16[8,64,256]{2,1,0:T(8,128)(2,1)}), bf16[8,64,256]{2,1,0:T(8,128)(2,1)S(1)}, u32[]{:S(2)}, u32[]{:S(2)}) async-start(bf16[8,64,256]{2,1,0:T(8,128)(2,1)} %copy.58), calls=%async_computation.2 | async-start | bytes 524288 | tf_op jit(solution)/shard_map/all_to_all | solution.py:215
  261.2 0.9 slice.123.refs_2_
  262.1 31.0 %all-to-all-done.2 = bf16[8,64,256]{2,1,0:T(8,128)(2,1)S(1)} async-done(((bf16[8,64,256]{2,1,0:T(8,128)(2,1)}), bf16[8,64,256]{2,1,0:T(8,128)(2,1)S(1)}, u32[]{:S(2)}, u32[]{:S(2)}) %all-to-all-start.2) | async-done | bytes 262176 | tf_op jit(solution)/shard_map/all_to_all | solution.py:215
  293.1 18.2 %all_gather.24 = bf16[256,256]{1,0:T(8,128)(2,1)S(1)} all-gather(bf16[64,256]{1,0:T(8,128)(2,1)S(1)} %reduce_sum.93), channel_id=1, replica_groups={{0,2,4,6},{8,10,12,14},{16,18,20,22},{24,26,28,30},{32,34,36,38},{40,42..., dimensions={0}, use_global_device_ids=true | all-gather | bytes 163840 | tf_op jit(solution)/shard_map/all_gather | solution.py:217
  311.5 0.8 fusion.12
  312.3 0.9 copy.61.refs_4_
  313.2 18.9 %query_partial.1 = (f32[512,256]{1,0:T(8,128)}, f32[512,128]{1,0:T(8,128)}) custom-call(s32[1]{0:T(128)} %bitcast.6.refs_0_, bf16[32,1808,128]{2,1,0:T(8,128)(2,1)} %bitcast.60, bf16[256,1280]{1,0:T(8,128)(2,1)} %slice.123.refs_2_, bf16[512,256]{1,0:T(8,128)(2,1)} %get-tuple-element.44.refs_3_, f32[512,1]{1,0:T(8,128)} %copy.61.refs_4_, ...), custom_call_target="tpu_custom_call" | custom-call | flops 4831838208 | bytes 14811136 | tf_op jit(solution)/shard_map/query_partial/pallas_call | solution.py:78
  332.1 1.1 constant_dynamic-update-slice_fusion.1
  333.2 1.0 constant_dynamic-update-slice_fusion
  334.6 1.5 collective-permute-done.1
  336.8 2.2 all_gather.27
  340.5 0.8 copy-done.1
  341.3 3.2 fusion
  344.6 126.0 %reduce-scatter.2.cloned.1.call-done = bf16[256,256]{0,1:T(8,128)(2,1)} async-done(((bf16[8192,256]{0,1:T(8,128)(2,1)}), bf16[256,256]{0,1:T(8,128)(2,1)}) %reduce-scatter.2.cloned.1.call-update) | async-done | bytes 131088 | tf_op jit(solution)/shard_map/reduce_scatter | solution.py:281
  470.5 1.6 fusion.18
  (104 shorter events, 6.9 us)
Async XLA Ops:
  6.5 1.8 copy-start
  6.6 99.6 %copy-start.4 = (bf16[256,1024]{1,0:T(8,128)(2,1)S(1)}, bf16[256,1024]{1,0:T(8,128)(2,1)}, u32[]{:S(2)}) copy-start(bf16[256,1024]{1,0:T(8,128)(2,1)} %param.33) | copy-start | bytes 1572868
  6.6 99.6 %copy-start.5 = (bf16[256,1024]{1,0:T(8,128)(2,1)S(1)}, bf16[256,1024]{1,0:T(8,128)(2,1)}, u32[]{:S(2)}) copy-start(bf16[256,1024]{1,0:T(8,128)(2,1)} %param.34) | copy-start | bytes 1572868
  6.6 99.5 %copy-start.13 = (s32[4]{0:T(128)S(1)}, s32[4]{0:T(128)}, u32[]{:S(2)}) copy-start(s32[4]{0:T(128)} %param.19) | copy-start | bytes 52
  6.6 306.6 %all-gather.5.cloned.1.call-start = ((), (), s32[]{:S(2)}) async-start(), calls=%async_computation.5 | async-start | bytes 15273984 | tf_op jit(solution)/shard_map/all_gather | solution.py:151
  7.6 1.3 collective-permute-start
  10.5 138.1 %copy-start.6 = (bf16[4,1280]{1,0:T(4,128)(2,1)S(1)}, bf16[4,1280]{1,0:T(4,128)(2,1)}, u32[]{:S(2)}) copy-start(bf16[4,1280]{1,0:T(4,128)(2,1)} %param.18) | copy-start | bytes 30724
  10.5 138.1 %copy-start.8 = (f32[1280]{0:T(1024)S(1)}, f32[1280]{0:T(1024)}, u32[]{:S(2)}) copy-start(f32[1280]{0:T(1024)} %param.27) | copy-start | bytes 15364
  10.5 138.5 %copy-start.9 = (f32[1280]{0:T(1024)S(1)}, f32[1280]{0:T(1024)}, u32[]{:S(2)}) copy-start(f32[1280]{0:T(1024)} %param.29) | copy-start | bytes 15364
  10.5 138.5 %copy-start.10 = (f32[1280]{0:T(1024)S(1)}, f32[1280]{0:T(1024)}, u32[]{:S(2)}) copy-start(f32[1280]{0:T(1024)} %param.28) | copy-start | bytes 15364
  91.9 118.8 %copy-start.7 = (bf16[256,256]{1,0:T(8,128)(2,1)S(1)}, bf16[256,256]{1,0:T(8,128)(2,1)}, u32[]{:S(2)}) copy-start(bf16[256,256]{1,0:T(8,128)(2,1)} %param.21) | copy-start | bytes 393220
  93.8 117.4 %copy-start.12 = (f32[256]{0:T(256)S(1)}, f32[256]{0:T(256)}, u32[]{:S(2)}) copy-start(f32[256]{0:T(256)} %param.31) | copy-start | bytes 3076
  94.6 53.9 %all-to-all-start = ((bf16[32,4,1280]{2,1,0:T(4,128)(2,1)}), bf16[32,4,1280]{2,1,0:T(4,128)(2,1)S(1)}, u32[]{:S(2)}, u32[]{:S(2)}) async-start(bf16[32,4,1280]{2,1,0:T(4,128)(2,1)} %reshape.248), calls=%async_computation | async-start | bytes 655360 | tf_op jit(solution)/shard_map/all_to_all | solution.py:184
  210.7 49.8 %copy-start.11 = (s32[256]{0:T(256)S(1)}, s32[256]{0:T(256)}, u32[]{:S(2)}) copy-start(s32[256]{0:T(256)} %param.20) | copy-start | bytes 3076
  211.3 0.7 copy-start.2
  253.5 39.6 %all-to-all-start.2 = ((bf16[8,64,256]{2,1,0:T(8,128)(2,1)}), bf16[8,64,256]{2,1,0:T(8,128)(2,1)S(1)}, u32[]{:S(2)}, u32[]{:S(2)}) async-start(bf16[8,64,256]{2,1,0:T(8,128)(2,1)} %copy.58), calls=%async_computation.2 | async-start | bytes 524288 | tf_op jit(solution)/shard_map/all_to_all | solution.py:215
  260.4 210.1 %reduce-scatter.2.cloned.1.call-start = ((), (), s32[]{:S(2)}) async-start(), calls=%async_computation.4 | async-start | bytes 4325376 | tf_op jit(solution)/shard_map/reduce_scatter | solution.py:281
  260.5 73.9 %collective-permute-start.2 = (s32[256]{0:T(256)S(1)}, s32[256]{0:T(256)S(1)}, u32[]{:S(2)}, u32[]{:S(2)}) collective-permute-start(s32[256]{0:T(256)S(1)} %copy-done.11), channel_id=1, source_target_pairs={{0,1},{1,0},{2,3},{3,2},{4,5},{5,4},{6,7},{7,6},{8,9},{9,8},{10,11... | collective-permute-start | bytes 3080 | tf_op jit(solution)/shard_map/ppermute | solution.py:21
  334.2 1.8 collective-permute-start.1
  339.1 2.2 copy-start.1
  344.5 126.0 %copy-start.3 = (f32[256,256]{1,0:T(8,128)S(1)}, f32[256,256]{1,0:T(8,128)}, u32[]{:S(2)}) copy-start(f32[256,256]{1,0:T(8,128)} %copy-done.2) | copy-start | bytes 786436
Sparse Core Ops, SparseCore 0:
  10.7 247.5 all-gather.4
  344.7 125.7 reduce-scatter.1
